TPU v7x, 256 devices: a whole 4x4x8 slice. The times are simulated.
256 devices in a mesh: wide: 64 (over z, y, core), narrow: 4 (over x).
Axes of the slice: x: 4, y: 4, z: 8, core: 2. Of those that a mesh axis runs over, the one named last changes fastest.
Arguments:
- coords_inner: float32 [2, 65536], P(None, ('wide', 'narrow')), may hold values from -1 to 1
- velocity: float32 [2, 65536], P(None, ('wide', 'narrow')), may hold values from -6 to 6
- source: float32 [65536], P(('wide', 'narrow')), may hold values from -6 to 6
- coords_edge: float32 [2, 32768], P(None, ('wide', 'narrow')), may hold values from -1 to 1
- flux_weight: float32 [2, 32768], P(None, ('wide', 'narrow')), may hold values from -6 to 6
- owner: int32 [32768, 1], P(('wide', 'narrow')), may hold values from 0 to 63; in each aligned block of 128 rows (0 to 127, 128 to 255, ...) at most 4 rows name the same one
- local_face: int32 [32768], P(('wide', 'narrow')), may hold values from 0 to 127
- w_first: float32 [2, 512], replicated, may hold values from -4 to 4
- b_first: float32 [512], replicated, may hold values from -3 to 3
- w_hidden: float32 [4, 512, 512], replicated, may hold values from -0.25 to 0.25
- b_hidden: float32 [4, 512], replicated, may hold values from -3 to 3
- w_last: float32 [512], replicated, may hold values from -0.25 to 0.25
Outputs:
- face_integral: float32 [8192], P('wide')
- grad_first: float32 [2, 512], replicated
- grad_hidden: float32 [4, 512, 512], replicated
- grad_last: float32 [512], replicated
Inputs may be any that keep to these rules, and one draw needn't show every extreme that they name: Among the 128 face points of one device no owner appears more than 4 times, and some owner appears exactly 4 times.
All inputs are finite; a program needn't handle non-finite values.
Results may differ from a plain program's by a relative error of at most 0.0003.
Values sent between devices are 32-bit elements; how exact they have to be, the bound alone decides.
A program may use at most 128 MiB of HBM per device.

v0:
```python
import math

import jax
import jax.numpy as jnp
from jax import lax
from jax.sharding import PartitionSpec as P

FACE_DEV = 128
penalty_weight = 4.0
BOTH = ("wide", "narrow")
precise = lax.Precision.HIGH


def forward(coords, direction, w_first, b_first, w_hidden, b_hidden, w_last):
    hidden = jnp.tanh(
        coords[0][:, None] * w_first[0][None] + coords[1][:, None] * w_first[1][None] + b_first
    )
    tangent = (1.0 - hidden * hidden) * (
        direction[0][:, None] * w_first[0][None] + direction[1][:, None] * w_first[1][None]
    )
    points = hidden.shape[0]
    kept = [(hidden, None, tangent)]
    for level in range(w_hidden.shape[0]):
        product = jnp.dot(
            jnp.concatenate([hidden, tangent], 0), w_hidden[level], precision=precise
        )
        hidden = jnp.tanh(product[:points] + b_hidden[level])
        slope = product[points:]
        tangent = (1.0 - hidden * hidden) * slope
        kept.append((hidden, slope, tangent))
    value = jnp.sum(hidden * w_last[None], 1)
    slopes = jnp.sum(tangent * w_last[None], 1)
    return value, slopes, kept


def backward(coords, direction, kept, hidden_cot, tangent_cot, w_first, w_hidden):
    grads = []
    for level in reversed(range(w_hidden.shape[0])):
        hidden, slope, _ = kept[level + 1]
        gate = 1.0 - hidden * hidden
        product_cot = gate * tangent_cot
        sum_cot = gate * (hidden_cot - 2.0 * hidden * slope * tangent_cot)
        cots = jnp.concatenate([sum_cot, product_cot], 0)
        below = jnp.concatenate([kept[level][0], kept[level][2]], 0)
        grads.append(
            lax.dot_general(below, cots, (((0,), (0,)), ((), ())), precision=precise)
        )
        down = lax.dot_general(cots, w_hidden[level], (((1,), (1,)), ((), ())), precision=precise)
        points = hidden.shape[0]
        hidden_cot, tangent_cot = down[:points], down[points:]
    hidden, _, _ = kept[0]
    gate = 1.0 - hidden * hidden
    start = direction[0][:, None] * w_first[0][None] + direction[1][:, None] * w_first[1][None]
    start_cot = gate * tangent_cot
    sum_cot = gate * (hidden_cot - 2.0 * hidden * start * tangent_cot)
    first = jnp.stack(
        [
            jnp.sum(coords[j][:, None] * sum_cot + direction[j][:, None] * start_cot, 0)
            for j in range(2)
        ]
    )
    return first, jnp.stack(grads[::-1], 0)


def local(
    coords_inner,
    velocity,
    source,
    coords_edge,
    flux_weight,
    owner,
    local_face,
    w_first,
    b_first,
    w_hidden,
    b_hidden,
    w_last,
):
    devices = lax.axis_size(BOTH)
    inner_rows = coords_inner.shape[1]
    edge_rows = coords_edge.shape[1]
    inner_scale = 2.0 / math.sqrt(inner_rows * devices)
    face_scale = 2.0 * penalty_weight / math.sqrt(FACE_DEV * lax.axis_size("wide"))
    net = (w_first, b_first, w_hidden, b_hidden, w_last)

    _, flux, kept_edge = forward(coords_edge, flux_weight, *net)
    face = owner[:, 0] * FACE_DEV + local_face
    mine = jnp.stack([flux, face.astype(jnp.float32)], 0)
    everyone = lax.all_gather(mine, BOTH)
    all_flux = everyone[:, 0].reshape(-1)
    all_face = everyone[:, 1].reshape(-1)

    def sums(wanted):
        return jnp.sum(
            jnp.where(wanted.astype(jnp.float32)[:, None] == all_face[None], all_flux[None], 0.0), 1
        )

    reached = sums(face)
    integral = sums(lax.axis_index("wide") * FACE_DEV + jnp.arange(FACE_DEV))

    value, slopes, kept_inner = forward(coords_inner, velocity, *net)
    inner_cot = inner_scale * (slopes + value - source)
    edge_cot = face_scale * reached

    coords = jnp.concatenate([coords_inner, coords_edge], 1)
    direction = jnp.concatenate([velocity, flux_weight], 1)
    kept = [
        tuple(None if a is None else jnp.concatenate([a, b], 0) for a, b in zip(one, two))
        for one, two in zip(kept_inner, kept_edge)
    ]
    hidden_out = jnp.concatenate([inner_cot, jnp.zeros_like(edge_cot)])[:, None]
    tangent_out = jnp.concatenate([inner_cot, edge_cot])[:, None]
    last = jnp.sum(hidden_out * kept[-1][0] + tangent_out * kept[-1][2], 0)
    first, hidden = backward(
        coords,
        direction,
        kept,
        hidden_out * w_last[None],
        tangent_out * w_last[None],
        w_first,
        w_hidden,
    )
    first, hidden, last = lax.psum((first, hidden, last), BOTH)
    return integral, first, hidden, last


def solution(mesh):
    points = P(None, BOTH)
    in_specs = (
        points,
        points,
        P(BOTH),
        points,
        points,
        P(BOTH, None),
        P(BOTH),
        P(),
        P(),
        P(),
        P(),
        P(),
    )
    out_specs = (P("wide"), P(), P(), P())
    return jax.shard_map(local, mesh=mesh, in_specs=in_specs, out_specs=out_specs, check_vma=False)
```

profile of v0, /device:TPU:1, one launch (start us, length us, event | category | flops | bytes accessed | tf_op | source)
XLA Modules:
  0.0 387.8 jit_solution(4115349576246029402)
XLA Ops:
  8.7 0.8 fusion.154
  9.5 0.9 fusion.153
  10.4 0.8 slice_bitcast_fusion.1
  11.1 0.8 add_tanh_fusion.1
  12.0 1.8 fusion.78
  13.9 2.0 fusion.74
  18.0 66.9 %all-gather.1 = f32[256,2,128]{2,1,0:T(2,128)S(1)} all-gather(f32[1,2,128]{2,1,0:T(2,128)S(1)} %maximum_bitcast_fusion), channel_id=2, replica_groups=mesh['wide'=64,'narrow'=4] {'wide','narrow'}, dimensions={0}, use_global_device_ids=true | all-gather | bytes 263168 | tf_op jit(solution)/shard_map/all_gather | solution.py:89
  85.1 4.7 %select_reduce_fusion = (f32[128]{0:T(128)S(1)}, f32[128]{0:T(128)}) fusion(f32[32768]{0:T(1024)S(1)} %bitcast.67, f32[32768]{0:T(1024)S(1)} %bitcast.66, f32[128]{0:T(128)S(1)} %get-tuple-element.74, f32[128]{0:T(128)S(1)} %get-tuple-element.75), kind=kLoop, calls=%fused_computation | loop fusion | flops 25165568 | bytes 264192 | tf_op jit(solution)/shard_map/reduce_sum | solution.py:94
  90.0 1.0 fusion.48
  91.3 1.1 fusion.52
  92.5 1.1 fusion.56
  93.7 1.1 fusion.60
  95.9 1.5 fusion.32
  97.4 1.7 fusion.47
  99.6 1.5 fusion.35
  101.1 1.5 fusion.46
  102.9 1.5 fusion.38
  104.4 1.5 fusion.45
  106.3 1.5 fusion.41
  107.8 2.5 pad_maximum_fusion
  111.0 2.7 fusion.44
  114.3 76.2 %all-reduce.1 = (f32[2,512]{1,0:T(2,128)}, f32[512]{0:T(512)}) all-reduce(f32[2,512]{1,0:T(2,128)S(1)} %pad_maximum_fusion.18, f32[512]{0:T(512)S(1)} %get-tuple-element.43), channel_id=1, replica_groups=mesh['wide'=64,'narrow'=4] {'wide','narrow'}, use_global_device_ids=true, to_apply=%region_7.8 | all-reduce | flops 1536 | bytes 12288 | tf_op jit(solution)/shard_map/psum | solution.py:123
  190.5 185.8 %all-reduce.4.cloned.1.call-done = f32[4,512,512]{2,1,0:T(8,128)} async-done(((f32[4,512,512]{2,1,0:T(8,128)}), f32[4,512,512]{2,1,0:T(8,128)}) %all-reduce.4.cloned.1.call-update) | async-done | bytes 4194320 | tf_op jit(solution)/shard_map/psum | solution.py:123
  376.3 4.6 %copy.19 = f32[4,512,512]{2,1,0:T(8,128)} copy(f32[4,512,512]{2,1,0:T(8,128)} %all-reduce.4.cloned.1.call-done) | data formatting | bytes 8388608
  (52 shorter events, 8.2 us)
Async XLA Ops:
  7.2 369.1 %all-reduce.4.cloned.1.call-start = ((), (), s32[]{:S(2)}) async-start(), calls=%async_computation | async-start | bytes 8388608 | tf_op jit(solution)/shard_map/psum | solution.py:123
  13.8 2.5 copy-start
  17.0 0.8 copy-start.8
  17.0 0.8 copy-start.9
  17.0 0.8 copy-start.1
  17.8 72.0 %copy-start.2 = (f32[512]{0:T(512)S(1)}, f32[512]{0:T(512)}, u32[]{:S(2)}) copy-start(f32[512]{0:T(512)} %param.20) | copy-start | bytes 6148
  94.8 0.7 copy-start.7
  110.3 0.7 copy-start.3
  110.3 0.7 copy-start.5
  110.3 0.7 copy-start.4
  110.3 0.7 copy-start.6
Sparse Core Ops, SparseCore 0:
  110.4 265.8 all-reduce.3
where the time goes:
time: 389 us; the launch traced here: 388 us
  waiting for transfers between devices  186 us (48%)
  blocking collectives  143 us (37%)
  matrix products  22.6 us (6%)
  between operations  14.4 us (4%)
  other arithmetic  11.6 us (3%)
  local copies, waits for them, and re-layouts  10.3 us (3%)
    psum x1, waiting for transfers between devices, local(): first, hidden, last = lax.psum((first, hidden, last), BOTH)  186 us
    psum x1, blocking collectives, local(): first, hidden, last = lax.psum((first, hidden, last), BOTH)  76.2 us
    all_gather x1, blocking collectives, local(): everyone = lax.all_gather(mine, BOTH)  66.9 us
    dot_general x8, matrix products, forward(): jnp.dot(jnp.concatenate([hidden, tangent], 0), w_hidden[level], precision...  9.34 us
  transfers between devices with their start and end apart: 1, of which 1 were waited for; matrix products, arithmetic and copies ran while one was open for 1% of the time, Pallas kernels for 0%

commit v1 on v0

--- a/solution.py
+++ b/solution.py
@@ -3,12 +3,342 @@
 import jax
 import jax.numpy as jnp
 from jax import lax
+from jax.experimental import pallas as pl
+from jax.experimental.pallas import tpu as pltpu
 from jax.sharding import PartitionSpec as P
+
+MESH = pl.DeviceIdType.MESH
 
 FACE_DEV = 128
 penalty_weight = 4.0
 BOTH = ("wide", "narrow")
 precise = lax.Precision.HIGH
+FACES = 64
+CHUNKS = 4
+TILES = 256
+
+
+def place():
+    wide = lax.axis_index("wide")
+    x = lax.axis_index("narrow")
+    return x, (wide // 2) % 4, wide // 8, wide % 2
+
+
+def device(x, y, z, core):
+    return {"wide": (z * 4 + y) * 2 + core, "narrow": x}
+
+
+def peers_x(d):
+    x, y, z, core = place()
+    return device((x + d) % 4, y, z, core)
+
+
+def peers_y(d):
+    x, y, z, core = place()
+    return device(x, (y + d) % 4, z, core)
+
+
+def peers_z(d):
+    x, y, z, core = place()
+    return device(x, y, (z + d) % 8, core)
+
+
+def partner():
+    x, y, z, core = place()
+    return device(x, y, z, 1 - core)
+
+
+def along_first(d):
+    x, y, z, core = place()
+    return device((x + d * (1 - core)) % 4, (y + d * core) % 4, z, core)
+
+
+def along_second(d):
+    x, y, z, core = place()
+    return device((x + d * core) % 4, (y + d * (1 - core)) % 4, z, core)
+
+
+def greet():
+    barrier = pltpu.get_barrier_semaphore()
+    others = (
+        [partner()]
+        + [peers_x(d) for d in range(1, 4)]
+        + [peers_y(d) for d in range(1, 4)]
+        + [peers_z(d) for d in range(1, 8)]
+    )
+    for other in others:
+        pl.semaphore_signal(barrier, inc=1, device_id=other, device_id_type=MESH)
+    pl.semaphore_wait(barrier, len(others))
+
+
+def remote(src, dst, sems, index, target):
+    return pltpu.make_async_remote_copy(
+        src_ref=src,
+        dst_ref=dst,
+        send_sem=sems[0].at[index],
+        recv_sem=sems[1].at[index],
+        device_id=target,
+        device_id_type=MESH,
+    )
+
+
+def faces_kernel(mine_ref, all_ref, row, got, send, recv):
+    x, y, z, core = place()
+    sems = (send, recv)
+    greet()
+    spot = lax.broadcasted_iota(jnp.int32, (8, 128), 0)
+    row[...] = jnp.where(spot == x, mine_ref[0:1, :], 0.0) + jnp.where(
+        spot == x + 4, mine_ref[1:2, :], 0.0
+    )
+    copies = [remote(row, got.at[d - 1], sems, d - 1, peers_x(d)) for d in range(1, 4)]
+    for copy in copies:
+        copy.start()
+    for copy in copies:
+        copy.wait()
+    at = core * 32 + z * 4
+    all_ref[at + y] = row[...] + got[0] + got[1] + got[2]
+    here = all_ref.at[at + y]
+    copies = [remote(here, here, sems, 2 + d, peers_y(d)) for d in range(1, 4)]
+    for copy in copies:
+        copy.start()
+    for copy in copies:
+        copy.wait()
+    here = all_ref.at[pl.ds(at, 4)]
+    copies = [remote(here, here, sems, 5 + d, peers_z(d)) for d in range(1, 8)]
+    for copy in copies:
+        copy.start()
+    for copy in copies:
+        copy.wait()
+    here = all_ref.at[pl.ds(core * 32, 32)]
+    copy = remote(here, here, sems, 13, partner())
+    copy.start()
+    copy.wait()
+
+
+def gather_faces(flux, face):
+    mine = jnp.stack([flux, face.astype(jnp.float32)], 0)
+    return pl.pallas_call(
+        faces_kernel,
+        out_shape=jax.ShapeDtypeStruct((FACES, 8, 128), jnp.float32),
+        in_specs=[pl.BlockSpec(memory_space=pltpu.VMEM)],
+        out_specs=pl.BlockSpec(memory_space=pltpu.VMEM),
+        scratch_shapes=[
+            pltpu.VMEM((8, 128), jnp.float32),
+            pltpu.VMEM((3, 8, 128), jnp.float32),
+            pltpu.SemaphoreType.DMA((14,)),
+            pltpu.SemaphoreType.DMA((14,)),
+        ],
+        compiler_params=pltpu.CompilerParams(collective_id=0, has_side_effects=True),
+    )(mine)
+
+
+def reduce_steps(k, grad, total, bufs, sems):
+    core_in, first_in, second_in, third_in, half, quarter, piece = bufs
+    x, y, z, core = place()
+    p1 = x * (1 - core) + y * core
+    p2 = y * (1 - core) + x * core
+    half_at = core * 128
+    first_at = half_at + p1 * 32
+    second_at = first_at + p2 * 8
+    base = k * 28
+    copies = {}
+
+    def launch(name, made):
+        copies[name] = made
+        for copy in made:
+            copy.start()
+
+    def settle(name):
+        for copy in copies[name]:
+            copy.wait()
+
+    def s0():
+        src = grad.at[k, pl.ds((1 - core) * 128, 128)]
+        launch("core", [remote(src, core_in.at[k], sems, base, partner())])
+
+    def s1():
+        settle("core")
+        half[k] = grad[k, pl.ds(half_at, 128)] + core_in[k]
+        launch(
+            "first",
+            [
+                remote(
+                    half.at[k, pl.ds(((p1 + d) % 4) * 32, 32)],
+                    first_in.at[k, d - 1],
+                    sems,
+                    base + d,
+                    along_first(d),
+                )
+                for d in range(1, 4)
+            ],
+        )
+
+    def s2():
+        settle("first")
+        quarter[k] = (half[k, pl.ds(p1 * 32, 32)] + first_in[k, 0]) + (
+            first_in[k, 1] + first_in[k, 2]
+        )
+        launch(
+            "second",
+            [
+                remote(
+                    quarter.at[k, pl.ds(((p2 + d) % 4) * 8, 8)],
+                    second_in.at[k, d - 1],
+                    sems,
+                    base + 3 + d,
+                    along_second(d),
+                )
+                for d in range(1, 4)
+            ],
+        )
+
+    def s3():
+        settle("second")
+        piece[k] = (quarter[k, pl.ds(p2 * 8, 8)] + second_in[k, 0]) + (
+            second_in[k, 1] + second_in[k, 2]
+        )
+        launch(
+            "third",
+            [
+                remote(piece.at[k, (z + d) % 8], third_in.at[k, d - 1], sems, base + 6 + d, peers_z(d))
+                for d in range(1, 8)
+            ],
+        )
+
+    def s4():
+        settle("third")
+        done = piece[k, z]
+        for d in range(7):
+            done = done + third_in[k, d]
+        total[k, second_at + z] = done
+        here = total.at[k, second_at + z]
+        launch("z", [remote(here, here, sems, base + 13 + d, peers_z(d)) for d in range(1, 8)])
+
+    def s5():
+        settle("z")
+        here = total.at[k, pl.ds(second_at, 8)]
+        launch("b", [remote(here, here, sems, base + 20 + d, along_second(d)) for d in range(1, 4)])
+
+    def s6():
+        settle("b")
+        here = total.at[k, pl.ds(first_at, 32)]
+        launch("a", [remote(here, here, sems, base + 23 + d, along_first(d)) for d in range(1, 4)])
+
+    def s7():
+        settle("a")
+        here = total.at[k, pl.ds(half_at, 128)]
+        launch("end", [remote(here, here, sems, base + 27, partner())])
+
+    def s8():
+        settle("end")
+
+    return [s0, s1, s2, s3, s4, s5, s6, s7, s8]
+
+
+def small_steps(small, small_out, got, part, sems, base):
+    x, y, z, core = place()
+    copies = {}
+
+    def launch(name, src, at, count, peer):
+        copies[name] = [
+            remote(src, got.at[at + d - 1], sems, base + at + d - 1, peer(d)) for d in range(1, count)
+        ]
+        for copy in copies[name]:
+            copy.start()
+
+    def ordered(mine, at, count, place_of):
+        result = None
+        for member in range(count):
+            value = jnp.where(place_of == member, mine, 0.0)
+            for d in range(1, count):
+                value = value + jnp.where((place_of - d) % count == member, got[at + d - 1], 0.0)
+            result = value if result is None else result + value
+        return result
+
+    def s0():
+        launch("core", small, 0, 2, lambda d: partner())
+
+    def s1():
+        copies["core"][0].wait()
+        part[0] = ordered(small[...], 0, 2, core)
+        launch("x", part.at[0], 1, 4, peers_x)
+
+    def s2():
+        for copy in copies["x"]:
+            copy.wait()
+        part[1] = ordered(part[0], 1, 4, x)
+        launch("y", part.at[1], 4, 4, peers_y)
+
+    def s3():
+        for copy in copies["y"]:
+            copy.wait()
+        part[2] = ordered(part[1], 4, 4, y)
+        launch("z", part.at[2], 7, 8, peers_z)
+
+    def s4():
+        for copy in copies["z"]:
+            copy.wait()
+        small_out[...] = ordered(part[2], 7, 8, z)
+
+    return [s0, s1, s2, s3, s4]
+
+
+def sum_kernel(
+    grad,
+    small,
+    total,
+    small_out,
+    core_in,
+    first_in,
+    second_in,
+    third_in,
+    half,
+    quarter,
+    piece,
+    small_in,
+    small_part,
+    send,
+    recv,
+):
+    sems = (send, recv)
+    greet()
+    bufs = (core_in, first_in, second_in, third_in, half, quarter, piece)
+    chunks = [reduce_steps(k, grad, total, bufs, sems) for k in range(CHUNKS)]
+    chunks.append(small_steps(small, small_out, small_in, small_part, sems, CHUNKS * 28))
+    for turn in range(CHUNKS + 9):
+        for k, steps in enumerate(chunks):
+            if 0 <= turn - k < len(steps):
+                steps[turn - k]()
+
+
+def sum_grads(grad, small):
+    tile = (8, 128)
+    count = CHUNKS * 28 + 14
+    return pl.pallas_call(
+        sum_kernel,
+        out_shape=(
+            jax.ShapeDtypeStruct((CHUNKS, TILES) + tile, jnp.float32),
+            jax.ShapeDtypeStruct((2,) + tile, jnp.float32),
+        ),
+        in_specs=[pl.BlockSpec(memory_space=pltpu.VMEM)] * 2,
+        out_specs=(pl.BlockSpec(memory_space=pltpu.VMEM),) * 2,
+        scratch_shapes=[
+            pltpu.VMEM((CHUNKS, 128) + tile, jnp.float32),
+            pltpu.VMEM((CHUNKS, 3, 32) + tile, jnp.float32),
+            pltpu.VMEM((CHUNKS, 3, 8) + tile, jnp.float32),
+            pltpu.VMEM((CHUNKS, 7) + tile, jnp.float32),
+            pltpu.VMEM((CHUNKS, 128) + tile, jnp.float32),
+            pltpu.VMEM((CHUNKS, 32) + tile, jnp.float32),
+            pltpu.VMEM((CHUNKS, 8) + tile, jnp.float32),
+            pltpu.VMEM((14, 2) + tile, jnp.float32),
+            pltpu.VMEM((3, 2) + tile, jnp.float32),
+            pltpu.SemaphoreType.DMA((count,)),
+            pltpu.SemaphoreType.DMA((count,)),
+        ],
+        compiler_params=pltpu.CompilerParams(
+            collective_id=1, has_side_effects=True, vmem_limit_bytes=40 * 2**20
+        ),
+    )(grad, small)
 
 
 def forward(coords, direction, w_first, b_first, w_hidden, b_hidden, w_last):
@@ -85,10 +415,9 @@
 
     _, flux, kept_edge = forward(coords_edge, flux_weight, *net)
     face = owner[:, 0] * FACE_DEV + local_face
-    mine = jnp.stack([flux, face.astype(jnp.float32)], 0)
-    everyone = lax.all_gather(mine, BOTH)
-    all_flux = everyone[:, 0].reshape(-1)
-    all_face = everyone[:, 1].reshape(-1)
+    everyone = gather_faces(flux, face)
+    all_flux = everyone[:, :4].reshape(-1)
+    all_face = everyone[:, 4:].reshape(-1)
 
     def sums(wanted):
         return jnp.sum(
@@ -120,8 +449,13 @@
         w_first,
         w_hidden,
     )
-    first, hidden, last = lax.psum((first, hidden, last), BOTH)
-    return integral, first, hidden, last
+    layers = hidden.shape[0]
+    tiles = hidden.reshape(layers, 64, 8, 4, 128).transpose(0, 3, 1, 2, 4)
+    small = jnp.concatenate([first.ravel(), last, jnp.zeros((512,), jnp.float32)])
+    tiles, small = sum_grads(tiles.reshape(layers, TILES, 8, 128), small.reshape(2, 8, 128))
+    hidden = tiles.reshape(layers, 4, 64, 8, 128).transpose(0, 2, 3, 1, 4).reshape(hidden.shape)
+    small = small.ravel()
+    return integral, small[:1024].reshape(2, 512), hidden, small[1024:1536]
 
 
 def solution(mesh):

time: 389 us -> 133 us (0.34)
  waiting for transfers between devices: 186 us -> 0 us
  blocking collectives: 143 us -> 0 us
  Pallas kernels: 0 us -> 85.7 us
  between operations: 14.4 us -> 1.08 us
    psum x1 -> x0, waiting for transfers between devices: 186 us -> none  [local(): first, hidden, last = lax.psum((first, hidden, last), BOTH)]
    pallas_call x0 -> x2, Pallas kernels: none -> 85.7 us  [the longest x1 60.6 us: sum_grads(): pl.pallas_call(sum_kernel, out_shape=(jax.ShapeDtypeStruct((CHUNKS, TILES...]
    psum x1 -> x0, blocking collectives: 76.2 us -> none  [local(): first, hidden, last = lax.psum((first, hidden, last), BOTH)]
    all_gather x1 -> x0, blocking collectives: 66.9 us -> none  [local(): everyone = lax.all_gather(mine, BOTH)]
    transpose x0 -> x1, local copies, waits for them, and re-layouts: none -> 4.8 us  [local(): tiles.reshape(layers, 4, 64, 8, 128).transpose(0, 2, 3, 1, 4)]
  transfers between devices with their start and end apart: 1 -> 0, of which waited for: 1 -> 0; matrix products, arithmetic and copies ran while one was open for 1% -> 0% of each run, Pallas kernels for 0% -> 0%
where the time goes in v1:
time: 133 us
  Pallas kernels  85.7 us (64%)
  matrix products  22.1 us (17%)
  local copies, waits for them, and re-layouts  12.1 us (9%)
  other arithmetic  11.8 us (9%)
    pallas_call x1, Pallas kernels, sum_grads(): pl.pallas_call(sum_kernel, out_shape=(jax.ShapeDtypeStruct((CHUNKS, TILES...  60.6 us
    pallas_call x1, Pallas kernels, gather_faces(): pl.pallas_call(faces_kernel, out_shape=jax.ShapeDtypeStruct((FACES, 8, 12...  25.1 us
    dot_general x8, matrix products, forward(): jnp.dot(jnp.concatenate([hidden, tangent], 0), w_hidden[level], precision...  10.5 us
    dot_general x4, matrix products, backward(): lax.dot_general(below, cots, (((0,), (0,)), ((), ())), precision=precise)  5.87 us
    dot_general x4, matrix products, backward(): lax.dot_general(cots, w_hidden[level], (((1,), (1,)), ((), ())), precisio...  5.76 us
    transpose x1, local copies, waits for them, and re-layouts, local(): tiles.reshape(layers, 4, 64, 8, 128).transpose(0, 2, 3, 1, 4)  4.8 us
    reduce_sum x1, other arithmetic, sums(): jnp.sum(jnp.where(wanted.astype(jnp.float32)[:, None] == all_face[None],...  4.68 us
    unnamed x27, local copies, waits for them, and re-layouts  3.01 us

profile of v1, /device:TPU:1, one launch (start us, length us, event | category | flops | bytes accessed | tf_op | source)
XLA Modules:
  0.0 132.8 jit_solution(3769355877454108218)
XLA Ops:
  1.3 0.8 fusion.154
  2.1 0.8 slice_bitcast_fusion.1
  2.9 0.8 add_tanh_fusion.1
  3.7 1.8 %fusion.78 = f32[256,512]{1,0:T(8,128)S(1)} fusion(f32[4,512,512]{2,1,0:T(8,128)} %param.21, f32[128,512]{1,0:T(8,128)S(1)} %get-tuple-element.61, f32[128,512]{1,0:T(8,128)S(1)} %get-tuple-element.60), kind=kOutput, calls=%fused_computation.80 | convolution fusion | flops 402784256 | bytes 2097152 | tf_op jit(solution)/shard_map/dot_general | solution.py:354
  5.7 2.0 %fusion.74 = f32[256,512]{1,0:T(8,128)S(1)} fusion(f32[4,512,512]{2,1,0:T(8,128)} %param.21, f32[128,512]{1,0:T(8,128)S(1)} %get-tuple-element.33, f32[128,512]{1,0:T(8,128)S(1)} %get-tuple-element.34), kind=kOutput, calls=%fused_computation.76 | convolution fusion | flops 402784256 | bytes 2097152 | tf_op jit(solution)/shard_map/dot_general | solution.py:354
  9.5 0.8 multiply_reduce_fusion.2
  10.8 25.1 %shard_map.147 = f32[64,8,128]{2,1,0:T(8,128)} custom-call(f32[2,128]{1,0:T(2,128)} %pad_maximum_fusion.19.mine_ref), custom_call_target="tpu_custom_call" | custom-call | tf_op jit(solution)/shard_map/pallas_call | solution.py:120
  36.0 1.1 fusion.152
  37.0 4.7 %select_reduce_fusion = (f32[128]{0:T(128)S(1)}, f32[128]{0:T(128)}) fusion(f32[32768]{0:T(1024)S(1)} %bitcast.84, f32[32768]{0:T(1024)S(1)} %bitcast.83, f32[128]{0:T(128)S(1)} %get-tuple-element.76, f32[128]{0:T(128)S(1)} %get-tuple-element.77), kind=kLoop, calls=%fused_computation | loop fusion | flops 25165568 | bytes 264192 | tf_op jit(solution)/shard_map/reduce_sum | solution.py:423
  42.0 2.4 %fusion.48 = f32[512,512]{1,0:T(8,128)S(1)} fusion(f32[256,512]{1,0:T(8,128)S(1)} %get-tuple-element.55, f32[256,512]{1,0:T(8,128)S(1)} %get-tuple-element.54, f32[4,512,512]{2,1,0:T(8,128)} %param.21), kind=kOutput, calls=%fused_computation.50 | convolution fusion | flops 805568512 | bytes 3145728 | tf_op jit(solution)/shard_map/dot_general | solution.py:354
  44.6 1.0 fusion.52
  45.8 1.0 fusion.56
  47.0 1.0 fusion.60
  49.4 1.5 %fusion.32 = f32[1,64,8,4,128]{4,2,3,1,0:T(8,128)S(1)} fusion(f32[128,512]{1,0:T(8,128)S(1)} %get-tuple-element.29, f32[256,512]{1,0:T(8,128)S(1)} %get-tuple-element.20, f32[128,512]{1,0:T(8,128)S(1)} %get-tuple-element.30, f32[256,512]{1,0:T(8,128)S(1)} %get-tuple-element.21, f32[384,512]{1,0:T(8,128)S(1)} %get-tuple-element.47, ...), kind=kOutput, calls=%fused_computation.40 | convolution fusion | flops 1209532416 | bytes 4194304 | tf_op jit(solution)/shard_map/dot_general | solution.py:376
  50.9 1.4 %fusion.47 = f32[768,512]{1,0:T(8,128)S(1)} fusion(f32[384,512]{1,0:T(8,128)S(1)} %get-tuple-element.47, f32[384,512]{1,0:T(8,128)S(1)} %get-tuple-element.46, f32[4,512,512]{2,1,0:T(8,128)S(1)} %copy-done.2), kind=kOutput, calls=%fused_computation.47 | convolution fusion | flops 1208352768 | bytes 4194304 | tf_op jit(solution)/shard_map/dot_general | solution.py:378
  52.7 1.5 %fusion.35 = f32[1,64,8,4,128]{4,2,3,1,0:T(8,128)S(1)} fusion(f32[128,512]{1,0:T(8,128)S(1)} %get-tuple-element.31, f32[256,512]{1,0:T(8,128)S(1)} %get-tuple-element.22, f32[128,512]{1,0:T(8,128)S(1)} %get-tuple-element.32, f32[256,512]{1,0:T(8,128)S(1)} %get-tuple-element.23, f32[384,512]{1,0:T(8,128)S(1)} %get-tuple-element.40, ...), kind=kOutput, calls=%fused_computation.41 | convolution fusion | flops 1209532416 | bytes 4194304 | tf_op jit(solution)/shard_map/dot_general | solution.py:376
  54.2 1.4 %fusion.46 = f32[768,512]{1,0:T(8,128)S(1)} fusion(f32[384,512]{1,0:T(8,128)S(1)} %get-tuple-element.40, f32[384,512]{1,0:T(8,128)S(1)} %get-tuple-element.39, f32[4,512,512]{2,1,0:T(8,128)S(1)} %copy-done.2), kind=kOutput, calls=%fused_computation.46 | convolution fusion | flops 1208352768 | bytes 4194304 | tf_op jit(solution)/shard_map/dot_general | solution.py:378
  56.0 1.5 %fusion.38 = f32[1,64,8,4,128]{4,2,3,1,0:T(8,128)S(1)} fusion(f32[128,512]{1,0:T(8,128)S(1)} %get-tuple-element.33, f32[256,512]{1,0:T(8,128)S(1)} %get-tuple-element.24, f32[128,512]{1,0:T(8,128)S(1)} %get-tuple-element.34, f32[256,512]{1,0:T(8,128)S(1)} %get-tuple-element.25, f32[384,512]{1,0:T(8,128)S(1)} %get-tuple-element.38, ...), kind=kOutput, calls=%fused_computation.42 | convolution fusion | flops 1209532416 | bytes 4194304 | tf_op jit(solution)/shard_map/dot_general | solution.py:376
  57.5 1.5 %fusion.45 = f32[768,512]{1,0:T(8,128)S(1)} fusion(f32[384,512]{1,0:T(8,128)S(1)} %get-tuple-element.38, f32[384,512]{1,0:T(8,128)S(1)} %get-tuple-element.37, f32[4,512,512]{2,1,0:T(8,128)S(1)} %copy-done.2), kind=kOutput, calls=%fused_computation.45 | convolution fusion | flops 1208352768 | bytes 4194304 | tf_op jit(solution)/shard_map/dot_general | solution.py:378
  59.3 1.5 %fusion.41 = f32[1,64,8,4,128]{4,2,3,1,0:T(8,128)S(1)} fusion(f32[128,512]{1,0:T(8,128)S(1)} %get-tuple-element.61, f32[256,512]{1,0:T(8,128)S(1)} %get-tuple-element.55, f32[128,512]{1,0:T(8,128)S(1)} %get-tuple-element.60, f32[256,512]{1,0:T(8,128)S(1)} %get-tuple-element.54, f32[384,512]{1,0:T(8,128)S(1)} %get-tuple-element.36, ...), kind=kOutput, calls=%fused_computation.43 | convolution fusion | flops 1209532416 | bytes 4194304 | tf_op jit(solution)/shard_map/dot_general | solution.py:376
  62.2 1.4 %fusion.44 = f32[768,512]{1,0:T(8,128)S(1)} fusion(f32[384,512]{1,0:T(8,128)S(1)} %get-tuple-element.36, f32[384,512]{1,0:T(8,128)S(1)} %get-tuple-element.35, f32[4,512,512]{2,1,0:T(8,128)S(1)} %copy-done.2), kind=kOutput, calls=%fused_computation.44 | convolution fusion | flops 1208352768 | bytes 4194304 | tf_op jit(solution)/shard_map/dot_general | solution.py:378
  64.3 60.6 %shard_map.148 = (f32[4,256,8,128]{3,2,1,0:T(8,128)S(1)}, f32[2,8,128]{2,1,0:T(8,128)S(1)}) custom-call(f32[4,256,8,128]{3,2,1,0:T(8,128)S(1)} %bitcast.79, f32[2,8,128]{2,1,0:T(8,128)S(1)} %maximum_bitcast_fusion.small), custom_call_target="tpu_custom_call" | custom-call | tf_op jit(solution)/shard_map/pallas_call | solution.py:317
  124.9 1.9 %copy-done = f32[4,256,8,128]{3,2,1,0:T(8,128)} copy-done((f32[4,256,8,128]{3,2,1,0:T(8,128)}, f32[4,256,8,128]{3,2,1,0:T(8,128)S(1)}, u32[]{:S(2)}) %copy-start) | copy-done | bytes 4194328
  127.4 4.8 %copy.29 = f32[4,64,8,4,128]{4,2,3,1,0:T(8,128)} copy(f32[4,64,8,4,128]{4,2,1,3,0:T(8,128)} %bitcast.80) | data formatting | bytes 8388608 | tf_op jit(solution)/shard_map/transpose | solution.py:456
  (60 shorter events, 9.5 us)
Async XLA Ops:
  0.6 4.9 %copy-start.6 = (f32[4,512]{1,0:T(4,128)S(1)}, f32[4,512]{1,0:T(4,128)}, u32[]{:S(2)}) copy-start(f32[4,512]{1,0:T(4,128)} %param.22) | copy-start | bytes 24580
  5.6 2.5 %copy-start.1 = (f32[4,512,512]{2,1,0:T(8,128)S(1)}, f32[4,512,512]{2,1,0:T(8,128)}, u32[]{:S(2)}) copy-start(f32[4,512,512]{2,1,0:T(8,128)} %param.21) | copy-start | bytes 12582916
  8.7 0.8 copy-start.4
  9.4 32.3 %copy-start.8 = (f32[2,256]{1,0:T(2,128)S(1)}, f32[2,256]{1,0:T(2,128)}, u32[]{:S(2)}) copy-start(f32[2,256]{1,0:T(2,128)} %param.12) | copy-start | bytes 6148
  9.4 32.3 %copy-start.7 = (f32[2,256]{1,0:T(2,128)S(1)}, f32[2,256]{1,0:T(2,128)}, u32[]{:S(2)}) copy-start(f32[2,256]{1,0:T(2,128)} %param.13) | copy-start | bytes 6148
  9.4 32.3 %copy-start.5 = (f32[512]{0:T(512)S(1)}, f32[512]{0:T(512)}, u32[]{:S(2)}) copy-start(f32[512]{0:T(512)} %param.20) | copy-start | bytes 6148
  42.0 2.6 %copy-start.2 = (f32[4,512,512]{2,1,0:T(8,128)S(1)}, f32[4,512,512]{2,1,0:T(8,128)}, u32[]{:S(2)}) copy-start(f32[4,512,512]{2,1,0:T(8,128)} %param.21) | copy-start | bytes 12582916
  48.0 0.7 copy-start.11
  48.0 1.0 copy-start.3
  61.5 0.7 copy-start.9
  61.5 0.7 copy-start.10
  124.9 1.9 %copy-start = (f32[4,256,8,128]{3,2,1,0:T(8,128)}, f32[4,256,8,128]{3,2,1,0:T(8,128)S(1)}, u32[]{:S(2)}) copy-start(f32[4,256,8,128]{3,2,1,0:T(8,128)S(1)} %get-tuple-element.7) | copy-start | bytes 12582916
